TPU v7x, 32 devices: a whole 2x2x4 slice. The times are simulated.
32 devices in a mesh: dp: 8 (over y, x, core), branch: 4 (over z).
Axes of the slice: x: 2, y: 2, z: 4, core: 2. Of those that a mesh axis runs over, the one named last changes fastest.
Arguments:
- image_hidden: bfloat16 [4096, 1024], P('dp', 'branch'), may hold values from -8 to 8
- text_hidden: bfloat16 [4096, 768], P('dp', 'branch'), may hold values from -8 to 8
- image_proj: bfloat16 [1024, 768], replicated, may hold values from -0.1875 to 0.1875
- text_proj: bfloat16 [768, 768], replicated, may hold values from -0.21650635 to 0.21650635
- log_inverse_sharpness: float32 [1], replicated, may hold values from 4 to 5.9
- partner: int32 [4096], replicated, may hold values from 0 to 4095, each once
Outputs:
- loss: float32 [1], replicated
- grad_log_scale: float32 [1], replicated
- grad_image_hidden: bfloat16 [4096, 1024], P('dp', 'branch')
- grad_text_hidden: bfloat16 [4096, 768], P('dp', 'branch')
- grad_image_proj: float32 [1024, 768], P('branch')
- grad_text_proj: float32 [768, 768], P('branch')
Inputs may be any that keep to these rules, and one draw needn't show every extreme that they name: `partner`: each text index appears exactly once.
All inputs are finite; a program needn't handle non-finite values.
Results may differ from a plain program's by a relative error of at most 0.0029.
The roundings to bfloat16 on the way count: a program that leaves them out, or rounds other values in their place, can miss the bound.
Values may be sent and summed in bfloat16 or wider, within the bound.
A program may use at most 64 MiB of HBM per device.

v0:
```python
import jax
import jax.numpy as jnp
from jax import lax
from jax.sharding import PartitionSpec as P

NORM_EPSILON = 1e-06


def normalize(raw_rows):
    lengths = jnp.sqrt(jnp.sum(raw_rows * raw_rows, axis=1, keepdims=True) + NORM_EPSILON)
    unit_rows = raw_rows / lengths
    return (unit_rows, lengths, unit_rows.astype(jnp.bfloat16))


def unnormalize(upstream, unit_rows, lengths):
    radial = jnp.sum(upstream * unit_rows, axis=1, keepdims=True)
    return ((upstream - unit_rows * radial) / lengths).astype(jnp.bfloat16)


def per_device(image_hidden, text_hidden, image_proj, text_proj, log_inverse_sharpness, partner):
    branch_count = lax.axis_size("branch")
    data_count = lax.axis_size("dp")
    branch_pos = lax.axis_index("branch")
    data_pos = lax.axis_index("dp")
    group_rows = image_hidden.shape[0]
    own_rows = group_rows // branch_count
    image_cols = image_hidden.shape[1]
    text_cols = text_hidden.shape[1]
    image_slab = lax.dynamic_slice_in_dim(image_proj, branch_pos * image_cols, image_cols, 0)
    text_slab = lax.dynamic_slice_in_dim(text_proj, branch_pos * text_cols, text_cols, 0)
    image_local, text_local = (
        lax.all_to_all(image_hidden, "branch", split_axis=0, concat_axis=1, tiled=True),
        lax.all_to_all(text_hidden, "branch", split_axis=0, concat_axis=1, tiled=True),
    )
    image_raw = jnp.dot(image_local, image_proj, preferred_element_type=jnp.float32)
    text_raw = jnp.dot(text_local, text_proj, preferred_element_type=jnp.float32)
    image_unit, image_length, image_emb = normalize(image_raw)
    text_unit, text_length, caption_feature_entries = normalize(text_raw)
    normalized_exponent_divisor = jnp.exp(log_inverse_sharpness[0])
    column_count = own_rows * data_count
    total_pairs = group_rows * data_count
    denominator = 2.0 * total_pairs
    group_emb = lax.all_gather(image_emb, "branch", axis=0, tiled=True)
    row_partner = lax.dynamic_slice_in_dim(partner, data_pos * group_rows, group_rows, 0)

    def column_ident(positions):
        return (positions // own_rows * branch_count + branch_pos) * own_rows + positions % own_rows

    block_piece = lax.all_gather(caption_feature_entries, "dp", axis=0, tiled=True)
    row_peak = jnp.full((group_rows,), -jnp.inf, jnp.float32)
    row_mass = jnp.zeros((group_rows,), jnp.float32)
    piece_width = block_piece.shape[0]
    matching_cosine_scores = normalized_exponent_divisor * lax.dot_general(
        group_emb, block_piece, (((1,), (1,)), ((), ())), preferred_element_type=jnp.float32
    )
    logits_kept = matching_cosine_scores
    column_ids = column_ident(jnp.arange(piece_width, dtype=jnp.int32))
    matched = row_partner[:, None] == column_ids[None, :]
    positive = jnp.sum(jnp.where(matched, matching_cosine_scores, 0.0), axis=1)
    new_peak = jnp.max(matching_cosine_scores, axis=1)
    row_mass = row_mass * jnp.exp(row_peak - new_peak) + jnp.sum(
        jnp.exp(matching_cosine_scores - new_peak[:, None]), axis=1
    )
    piece_peak = jnp.max(matching_cosine_scores, axis=0)
    piece_mass = jnp.sum(jnp.exp(matching_cosine_scores - piece_peak[None, :]), axis=0)
    column_peak = piece_peak
    column_mass = piece_mass
    (
        retained_text_rows,
        matching_cosine_scores,
        row_peak,
        row_mass,
        positive,
        column_peak,
        column_mass,
    ) = (block_piece, logits_kept, new_peak, row_mass, positive, column_peak, column_mass)
    row_highest = lax.pmax(row_peak, "branch")
    row_mass, positive = lax.psum((row_mass * jnp.exp(row_peak - row_highest), positive), "branch")
    row_peak = row_highest
    column_highest = lax.pmax(column_peak, "dp")
    column_mass = lax.psum(column_mass * jnp.exp(column_peak - column_highest), "dp")
    column_peak = column_highest
    row_lse = row_peak + jnp.log(row_mass)
    col_lse = column_peak + jnp.log(column_mass)
    column_ids = column_ident(jnp.arange(column_count, dtype=jnp.int32))
    matched = (row_partner[:, None] == column_ids[None, :]).astype(jnp.float32)
    weights = (
        jnp.exp(matching_cosine_scores - row_lse[:, None])
        + jnp.exp(matching_cosine_scores - col_lse[None, :])
        - 2.0 * matched
    ) / denominator
    scale_part = jnp.sum(weights * matching_cosine_scores)
    reduced_width_parameters = weights.astype(jnp.bfloat16)
    picture_projection_matrix = lax.psum_scatter(
        normalized_exponent_divisor
        * jnp.dot(reduced_width_parameters, retained_text_rows, preferred_element_type=jnp.float32),
        "branch",
        scatter_dimension=0,
        tiled=True,
    )
    text_up = lax.psum_scatter(
        normalized_exponent_divisor
        * lax.dot_general(
            reduced_width_parameters,
            group_emb,
            (((0,), (0,)), ((), ())),
            preferred_element_type=jnp.float32,
        ),
        "dp",
        scatter_dimension=0,
        tiled=True,
    )
    image_down = unnormalize(picture_projection_matrix, image_unit, image_length)
    text_down = unnormalize(text_up, text_unit, text_length)
    image_gathered, text_gathered = (
        lax.all_gather(image_down, "branch", axis=0, tiled=True),
        lax.all_gather(text_down, "branch", axis=0, tiled=True),
    )
    grad_image_hidden = jnp.dot(
        image_gathered, image_slab.T, preferred_element_type=jnp.float32
    ).astype(jnp.bfloat16)
    grad_text_hidden = jnp.dot(
        text_gathered, text_slab.T, preferred_element_type=jnp.float32
    ).astype(jnp.bfloat16)
    image_weight = lax.dot_general(
        image_hidden, image_gathered, (((0,), (0,)), ((), ())), preferred_element_type=jnp.float32
    )
    text_weight = lax.dot_general(
        text_hidden, text_gathered, (((0,), (0,)), ((), ())), preferred_element_type=jnp.float32
    )
    grad_image_proj, grad_text_proj = lax.psum((image_weight, text_weight), "dp")
    own_row_terms = lax.dynamic_slice_in_dim(
        row_lse - 2.0 * positive, branch_pos * own_rows, own_rows, 0
    )
    own_col_terms = lax.dynamic_slice_in_dim(col_lse, data_pos * own_rows, own_rows, 0)
    loss_part = (jnp.sum(own_row_terms) + jnp.sum(own_col_terms)) / denominator
    loss_total, scale_total = lax.psum((loss_part, scale_part), ("dp", "branch"))
    return (
        loss_total.reshape(1),
        scale_total.reshape(1),
        grad_image_hidden,
        grad_text_hidden,
        grad_image_proj,
        grad_text_proj,
    )


def solution(mesh):
    placed = (P("dp", "branch"), P("dp", "branch"), P(), P(), P(), P())
    return jax.shard_map(
        per_device,
        mesh=mesh,
        in_specs=placed,
        out_specs=(
            P(),
            P(),
            P("dp", "branch"),
            P("dp", "branch"),
            P("branch", None),
            P("branch", None),
        ),
        check_vma=False,
    )
```

profile of v0, /device:TPU:0, one launch (start us, length us, event | category | flops | bytes accessed | tf_op | source)
XLA Modules:
  0.0 283.1 jit_solution(11487178637805667783)
XLA Ops:
  8.3 13.6 %all_to_all.38 = bf16[4,128,192]{1,2,0:T(8,128)(2,1)S(1)} all-to-all(bf16[4,128,192]{1,2,0:T(8,128)(2,1)S(1)} %copy_bitcast_fusion), channel_id=1, replica_groups=mesh['dp'=8,'branch'=4] {'branch'}, dimensions={0} | all-to-all | bytes 393216 | tf_op jit(solution)/shard_map/all_to_all | solution.py:33
  24.5 3.4 %all-to-all-start = ((bf16[4,128,256]{2,1,0:T(8,128)(2,1)}), bf16[4,128,256]{2,1,0:T(8,128)(2,1)S(1)}, u32[]{:S(2)}, u32[]{:S(2)}) async-start(bf16[4,128,256]{2,1,0:T(8,128)(2,1)} %bitcast.1), calls=%async_computation | async-start | bytes 524288 | tf_op jit(solution)/shard_map/all_to_all | solution.py:32
  29.4 6.6 %all-to-all-done = bf16[4,128,256]{2,1,0:T(8,128)(2,1)S(1)} async-done(((bf16[4,128,256]{2,1,0:T(8,128)(2,1)}), bf16[4,128,256]{2,1,0:T(8,128)(2,1)S(1)}, u32[]{:S(2)}, u32[]{:S(2)}) %all-to-all-start) | async-done | bytes 262176 | tf_op jit(solution)/shard_map/all_to_all | solution.py:32
  36.8 17.6 %all_gather.12 = bf16[512,768]{1,0:T(8,128)(2,1)S(1)} all-gather(bf16[128,768]{1,0:T(8,128)(2,1)S(1)} %fusion.19), channel_id=1, replica_groups=mesh['dp'=8,'branch'=4] {'branch'}, dimensions={0}, use_global_device_ids=true | all-gather | bytes 983040 | tf_op jit(solution)/shard_map/all_gather | solution.py:43
  54.4 3.8 %fusion.23 = (f32[1024]{0:T(1024)S(1)}, f32[512]{0:T(512)S(1)}, f32[512,1024]{1,0:T(8,128)}) fusion(bf16[512,768]{1,0:T(8,128)(2,1)S(1)} %all_gather.12, bf16[1024,768]{1,0:T(8,128)(2,1)} %all-gather.2.cloned.1.call-done, f32[]{:T(128)} %bitcast), kind=kOutput, calls=%fused_computation.55 | convolution fusion | flops 806877696 | bytes 4462596 | tf_op jit(solution)/shard_map/dot_general | solution.py:53
  58.2 10.3 %pmax.14 = f32[512]{0:T(512)S(1)} all-reduce(f32[512]{0:T(512)S(1)} %get-tuple-element.35), channel_id=1, replica_groups=mesh['dp'=8,'branch'=4] {'branch'}, use_global_device_ids=true, to_apply=%region_3.4 | all-reduce | flops 512 | bytes 4096 | tf_op jit(solution)/shard_map/pmax | solution.py:77
  68.5 11.8 %pmax.15 = f32[1024]{0:T(1024)S(1)} all-reduce(f32[1024]{0:T(1024)S(1)} %get-tuple-element.34), channel_id=1, replica_groups=mesh['dp'=8,'branch'=4] {'dp'}, use_global_device_ids=true, to_apply=%region_10.11 | all-reduce | flops 1024 | bytes 8192 | tf_op jit(solution)/shard_map/pmax | solution.py:80
  80.3 2.3 exponential_reduce_fusion
  82.7 11.9 %psum.51 = f32[1024]{0:T(1024)S(1)} all-reduce(f32[1024]{0:T(1024)S(1)} %exponential_multiply_fusion), channel_id=1, replica_groups=mesh['dp'=8,'branch'=4] {'dp'}, use_global_device_ids=true, to_apply=%region_12.13 | all-reduce | flops 1024 | bytes 8192 | tf_op jit(solution)/shard_map/psum | solution.py:81
  94.6 8.4 %psum.49 = f32[512]{0:T(512)S(1)} all-reduce(f32[512]{0:T(512)S(1)} %exponential_multiply_fusion.1), channel_id=1, replica_groups=mesh['dp'=8,'branch'=4] {'branch'}, use_global_device_ids=true, to_apply=%region_5.6 | all-reduce | flops 512 | bytes 4096 | tf_op jit(solution)/shard_map/psum | solution.py:78
  103.0 4.8 %convolution_multiply_fusion.2 = f32[512,768]{1,0:T(8,128)} fusion(bf16[1024,768]{1,0:T(8,128)(2,1)} %all-gather.2.cloned.1.call-done, f32[]{:T(128)} %bitcast, f32[512,1024]{1,0:T(8,128)} %get-tuple-element.44, f32[1024]{0:T(1024)S(1)} %log_add_fusion, f32[512]{0:T(512)S(1)} %log_add_fusion.1, s32[1024]{0:T(1024)S(1)} %fusion.15, s32[512]{0:T(512)S(1)} %dynamic_slice.15), kind=kOutput, calls=%fused_computation.11 | convolution fusion | flops 809893888 | bytes 5255172 | tf_op jit(solution)/shard_map/dot_general | solution.py:96
  107.9 4.8 %convolution_multiply_fusion = f32[1024,768]{1,0:T(8,128)} fusion(bf16[512,768]{1,0:T(8,128)(2,1)S(1)} %all_gather.12, f32[]{:T(128)} %bitcast, f32[512,1024]{1,0:T(8,128)} %get-tuple-element.44, f32[1024]{0:T(1024)S(1)} %log_add_fusion, f32[512]{0:T(512)S(1)} %log_add_fusion.1, s32[1024]{0:T(1024)S(1)} %fusion.15, s32[512]{0:T(512)S(1)} %dynamic_slice.15), kind=kOutput, calls=%fused_computation.9 | convolution fusion | flops 810287104 | bytes 6041604 | tf_op jit(solution)/shard_map/dot_general | solution.py:103
  113.5 3.6 %multiply_reduce_fusion = (f32[]{:T(128)}, f32[512]{0:T(512)S(1)}) fusion(f32[512,1024]{1,0:T(8,128)} %get-tuple-element.44, f32[1024]{0:T(1024)S(1)} %log_add_fusion, f32[512]{0:T(512)S(1)} %log_add_fusion.1, s32[1024]{0:T(1024)S(1)} %fusion.15, s32[512]{0:T(512)S(1)} %dynamic_slice.15), kind=kLoop, calls=%fused_computation.5 | loop fusion | flops 5766655 | bytes 2111492 | tf_op jit(solution)/shard_map/reduce_sum | solution.py:92
  117.1 11.2 %psum.50 = f32[512]{0:T(512)S(1)} all-reduce(f32[512]{0:T(512)S(1)} %get-tuple-element.31), channel_id=1, replica_groups=mesh['dp'=8,'branch'=4] {'branch'}, use_global_device_ids=true, to_apply=%region_7.8 | all-reduce | flops 512 | bytes 4096 | tf_op jit(solution)/shard_map/psum | solution.py:78
  128.3 14.0 %reduce-scatter.3.cloned.1.call-done = f32[128,768]{1,0:T(8,128)} async-done(((f32[512,768]{1,0:T(8,128)}), f32[128,768]{1,0:T(8,128)}) %reduce-scatter.3.cloned.1.call-update) | async-done | bytes 393232 | tf_op jit(solution)/shard_map/reduce_scatter | solution.py:94
  144.6 17.9 %all_gather.14 = bf16[512,768]{1,0:T(8,128)(2,1)S(1)} all-gather(bf16[128,768]{1,0:T(8,128)(2,1)S(1)} %divide_convert_fusion.1), channel_id=1, replica_groups=mesh['dp'=8,'branch'=4] {'branch'}, dimensions={0}, use_global_device_ids=true | all-gather | bytes 983040 | tf_op jit(solution)/shard_map/all_gather | solution.py:116
  162.5 2.2 convolution_bitcast_fusion
  164.8 25.9 %reduce-scatter.5.cloned.1.call-done = f32[128,768]{1,0:T(8,128)} async-done(((f32[1024,768]{1,0:T(8,128)}), f32[128,768]{1,0:T(8,128)}) %reduce-scatter.5.cloned.1.call-update) | async-done | bytes 393232 | tf_op jit(solution)/shard_map/reduce_scatter | solution.py:101
  193.0 19.6 %all_gather.15 = bf16[512,768]{1,0:T(8,128)(2,1)S(1)} all-gather(bf16[128,768]{1,0:T(8,128)(2,1)S(1)} %divide_convert_fusion), channel_id=1, replica_groups=mesh['dp'=8,'branch'=4] {'branch'}, dimensions={0}, use_global_device_ids=true | all-gather | bytes 983040 | tf_op jit(solution)/shard_map/all_gather | solution.py:117
  212.5 2.1 convolution_bitcast_fusion.1
  216.6 38.5 %all-reduce = (f32[1]{0:T(128)}, f32[1]{0:T(128)}) all-reduce(f32[1]{0:T(128)} %bitcast.6, f32[1]{0:T(128)} %bitcast.7), channel_id=1, replica_groups=mesh['dp'=8,'branch'=4] {'dp','branch'}, use_global_device_ids=true, to_apply=%region_14.15 | all-reduce | flops 2 | bytes 16 | tf_op jit(solution)/shard_map/psum | solution.py:137
  256.2 2.0 convolution_convert_fusion.1
  258.3 14.1 %all-reduce.4.cloned.1.call-done = (f32[256,768]{0,1:T(8,128)}, f32[192,768]{1,0:T(8,128)}) async-done(((f32[256,768]{0,1:T(8,128)}, f32[192,768]{1,0:T(8,128)}), (f32[256,768]{0,1:T(8,128)}, f32[192,768]{1,0:T(8,128)})) %all-reduce.4.cloned.1.call-update) | async-done | bytes 1376272 | tf_op jit(solution)/shard_map/psum | solution.py:131
  272.3 2.3 copy.19
  (34 shorter events, 14.4 us)
Async XLA Ops:
  7.2 29.0 %copy-start = (bf16[1024,768]{1,0:T(8,128)(2,1)S(1)}, bf16[1024,768]{1,0:T(8,128)(2,1)}, u32[]{:S(2)}) copy-start(bf16[1024,768]{1,0:T(8,128)(2,1)} %param.8) | copy-start | bytes 4718596
  7.2 47.2 %all-gather.2.cloned.1.call-start = ((), (), s32[]{:S(2)}) async-start(), calls=%async_computation.4 | async-start | bytes 1769472 | tf_op jit(solution)/shard_map/all_gather | solution.py:49
  24.5 11.6 %all-to-all-start = ((bf16[4,128,256]{2,1,0:T(8,128)(2,1)}), bf16[4,128,256]{2,1,0:T(8,128)(2,1)S(1)}, u32[]{:S(2)}, u32[]{:S(2)}) async-start(bf16[4,128,256]{2,1,0:T(8,128)(2,1)} %bitcast.1), calls=%async_computation | async-start | bytes 524288 | tf_op jit(solution)/shard_map/all_to_all | solution.py:32
  27.9 114.4 %reduce-scatter.3.cloned.1.call-start = ((), (), s32[]{:S(2)}) async-start(), calls=%async_computation.5 | async-start | bytes 1966080 | tf_op jit(solution)/shard_map/reduce_scatter | solution.py:94
  107.8 82.8 %reduce-scatter.5.cloned.1.call-start = ((), (), s32[]{:S(2)}) async-start(), calls=%async_computation.6 | async-start | bytes 3538944 | tf_op jit(solution)/shard_map/reduce_scatter | solution.py:101
  112.8 159.6 %all-reduce.4.cloned.1.call-start = ((), (), s32[]{:S(2)}) async-start(), calls=%async_computation.7 | async-start | bytes 2752512 | tf_op jit(solution)/shard_map/psum | solution.py:131
Sparse Core Ops, SparseCore 0:
  24.6 24.6 all-gather.1
  108.0 34.2 reduce-scatter.2
  145.7 44.9 reduce-scatter.4
  214.8 57.5 all-reduce.3
where the time goes:
time: 284 us; the launch traced here: 283 us
  blocking collectives  161 us (57%)
  waiting for transfers between devices  60.6 us (21%)
  matrix products  23.1 us (8%)
  between operations  15.9 us (6%)
  other arithmetic  12.9 us (5%)
  local copies, waits for them, and re-layouts  6.21 us (2%)
  starting transfers between devices  3.58 us (1%)
    psum x1, blocking collectives, per_device(): lax.psum((loss_part, scale_part), ('dp', 'branch'))  38.5 us
    reduce_scatter x1, waiting for transfers between devices, per_device(): lax.psum_scatter(normalized_exponent_divisor * lax.dot_general(reduced_wi...  25.9 us
    all_gather x1, blocking collectives, per_device(): lax.all_gather(text_down, 'branch', axis=0, tiled=True)  19.6 us
    psum x2, blocking collectives, per_device(): lax.psum((row_mass * jnp.exp(row_peak - row_highest), positive), 'branch')  19.6 us
    all_gather x1, blocking collectives, per_device(): lax.all_gather(image_down, 'branch', axis=0, tiled=True)  17.9 us
    all_gather x1, blocking collectives, per_device(): group_emb = lax.all_gather(image_emb, 'branch', axis=0, tiled=True)  17.6 us
    psum x1, waiting for transfers between devices, per_device(): lax.psum((image_weight, text_weight), 'dp')  14.1 us
    reduce_scatter x1, waiting for transfers between devices, per_device(): lax.psum_scatter(normalized_exponent_divisor * jnp.dot(reduced_width_para...  14 us
  transfers between devices with their start and end apart: 5, of which 4 were waited for; matrix products, arithmetic and copies ran while one was open for 7% of the time, Pallas kernels for 0%

commit v1 on v0

--- a/solution.py
+++ b/solution.py
@@ -40,7 +40,14 @@
     column_count = own_rows * data_count
     total_pairs = group_rows * data_count
     denominator = 2.0 * total_pairs
-    group_emb = lax.all_gather(image_emb, "branch", axis=0, tiled=True)
+    ring = [image_emb]
+    for hop in range(3):
+        ring.append(lax.ppermute(ring[-1], "branch", [(dev, (dev + 1) % 4) for dev in range(4)]))
+    group_emb = jnp.roll(
+        jnp.concatenate(ring[::-1], axis=0),
+        (lax.axis_index("branch") + 1) * ring[0].shape[0],
+        axis=0,
+    )
     row_partner = lax.dynamic_slice_in_dim(partner, data_pos * group_rows, group_rows, 0)
 
     def column_ident(positions):

time: 284 us -> 291 us (1.025)
  waiting for transfers between devices: 60.6 us -> 83 us
  blocking collectives: 161 us -> 141 us
  local copies, waits for them, and re-layouts: 6.21 us -> 10.4 us
    ppermute x0 -> x3, waiting for transfers between devices: none -> 22.1 us  [per_device(): lax.ppermute(ring[-1], 'branch', [(dev, (dev + 1) % 4) for dev in range(4)])]
    all_gather x1 -> x0, blocking collectives: 17.6 us -> none  [per_device(): group_emb = lax.all_gather(image_emb, 'branch', axis=0, tiled=True)]
    unnamed x4 -> x14, local copies, waits for them, and re-layouts: 4.21 us -> 8.34 us
  transfers between devices with their start and end apart: 5 -> 8, of which waited for: 4 -> 7; matrix products, arithmetic and copies ran while one was open for 7% -> 9% of each run, Pallas kernels for 0% -> 0%
where the time goes in v1:
time: 291 us; the launch traced here: 290 us
  blocking collectives  141 us (48%)
  waiting for transfers between devices  83 us (29%)
  matrix products  21.6 us (7%)
  between operations  15.9 us (5%)
  other arithmetic  14.5 us (5%)
  local copies, waits for them, and re-layouts  10.4 us (4%)
  starting transfers between devices  3.81 us (1%)
    psum x1, blocking collectives, per_device(): lax.psum((loss_part, scale_part), ('dp', 'branch'))  38.5 us
    reduce_scatter x1, waiting for transfers between devices, per_device(): lax.psum_scatter(normalized_exponent_divisor * lax.dot_general(reduced_wi...  26.8 us
    ppermute x3, waiting for transfers between devices, per_device(): lax.ppermute(ring[-1], 'branch', [(dev, (dev + 1) % 4) for dev in range(4)])  22.1 us
    all_gather x1, blocking collectives, per_device(): lax.all_gather(text_down, 'branch', axis=0, tiled=True)  19.6 us
    psum x2, blocking collectives, per_device(): lax.psum((row_mass * jnp.exp(row_peak - row_highest), positive), 'branch')  19.5 us
    all_gather x1, blocking collectives, per_device(): lax.all_gather(image_down, 'branch', axis=0, tiled=True)  17.9 us
    reduce_scatter x1, waiting for transfers between devices, per_device(): lax.psum_scatter(normalized_exponent_divisor * jnp.dot(reduced_width_para...  14.5 us
    psum x1, waiting for transfers between devices, per_device(): lax.psum((image_weight, text_weight), 'dp')  14 us
  transfers between devices with their start and end apart: 8, of which 7 were waited for; matrix products, arithmetic and copies ran while one was open for 9% of the time, Pallas kernels for 0%

profile of v1, /device:TPU:0, one launch (start us, length us, event | category | flops | bytes accessed | tf_op | source)
XLA Modules:
  0.0 290.2 jit_solution(16731163911076620700)
XLA Ops:
  8.3 13.6 %all_to_all.38 = bf16[4,128,192]{1,2,0:T(8,128)(2,1)S(1)} all-to-all(bf16[4,128,192]{1,2,0:T(8,128)(2,1)S(1)} %copy_bitcast_fusion), channel_id=1, replica_groups=mesh['dp'=8,'branch'=4] {'branch'}, dimensions={0} | all-to-all | bytes 393216 | tf_op jit(solution)/shard_map/all_to_all | solution.py:33
  21.9 3.4 %all-to-all-start = ((bf16[4,128,256]{2,1,0:T(8,128)(2,1)}), bf16[4,128,256]{2,1,0:T(8,128)(2,1)S(1)}, u32[]{:S(2)}, u32[]{:S(2)}) async-start(bf16[4,128,256]{2,1,0:T(8,128)(2,1)} %bitcast.30), calls=%async_computation | async-start | bytes 524288 | tf_op jit(solution)/shard_map/all_to_all | solution.py:32
  27.9 5.5 %all-to-all-done = bf16[4,128,256]{2,1,0:T(8,128)(2,1)S(1)} async-done(((bf16[4,128,256]{2,1,0:T(8,128)(2,1)}), bf16[4,128,256]{2,1,0:T(8,128)(2,1)S(1)}, u32[]{:S(2)}, u32[]{:S(2)}) %all-to-all-start) | async-done | bytes 262176 | tf_op jit(solution)/shard_map/all_to_all | solution.py:32
  34.5 7.4 %collective-permute-done = bf16[128,768]{1,0:T(8,128)(2,1)S(1)} collective-permute-done((bf16[128,768]{1,0:T(8,128)(2,1)S(1)}, bf16[128,768]{1,0:T(8,128)(2,1)S(1)}, u32[]{:S(2)}, u32[]{:S(2)}) %collective-permute-start) | collective-permute-done | bytes 196640 | tf_op jit(solution)/shard_map/ppermute | solution.py:45
  41.9 8.7 %collective-permute-done.1 = bf16[128,768]{1,0:T(8,128)(2,1)S(1)} collective-permute-done((bf16[128,768]{1,0:T(8,128)(2,1)S(1)}, bf16[128,768]{1,0:T(8,128)(2,1)S(1)}, u32[]{:S(2)}, u32[]{:S(2)}) %collective-permute-start.1) | collective-permute-done | bytes 196640 | tf_op jit(solution)/shard_map/ppermute | solution.py:45
  52.1 6.0 %collective-permute-done.2 = bf16[128,768]{1,0:T(8,128)(2,1)S(1)} collective-permute-done((bf16[128,768]{1,0:T(8,128)(2,1)S(1)}, bf16[128,768]{1,0:T(8,128)(2,1)S(1)}, u32[]{:S(2)}, u32[]{:S(2)}) %collective-permute-start.2) | collective-permute-done | bytes 196640 | tf_op jit(solution)/shard_map/ppermute | solution.py:45
  63.8 4.0 %fusion.27 = (f32[1024]{0:T(1024)S(1)}, f32[512]{0:T(512)S(1)}, f32[512,1024]{1,0:T(8,128)}) fusion(bf16[1024,768]{1,0:T(8,128)(2,1)} %all-gather.2.cloned.1.call-done, bf16[1024,768]{1,0:T(8,128)(2,1)} %constant_dynamic-update-slice_fusion, s32[]{:T(128)S(6)} %select_n.55, f32[]{:T(128)} %bitcast), kind=kOutput, calls=%fused_computation.67 | convolution fusion | flops 806877696 | bytes 4463108 | tf_op jit(solution)/shard_map/dot_general | solution.py:60
  67.8 8.3 %pmax.14 = f32[512]{0:T(512)S(1)} all-reduce(f32[512]{0:T(512)S(1)} %get-tuple-element.35), channel_id=1, replica_groups=mesh['dp'=8,'branch'=4] {'branch'}, use_global_device_ids=true, to_apply=%region_3.4 | all-reduce | flops 512 | bytes 4096 | tf_op jit(solution)/shard_map/pmax | solution.py:84
  76.2 11.8 %pmax.15 = f32[1024]{0:T(1024)S(1)} all-reduce(f32[1024]{0:T(1024)S(1)} %get-tuple-element.34), channel_id=1, replica_groups=mesh['dp'=8,'branch'=4] {'dp'}, use_global_device_ids=true, to_apply=%region_10.11 | all-reduce | flops 1024 | bytes 8192 | tf_op jit(solution)/shard_map/pmax | solution.py:87
  88.0 2.3 exponential_reduce_fusion
  90.3 11.9 %psum.51 = f32[1024]{0:T(1024)S(1)} all-reduce(f32[1024]{0:T(1024)S(1)} %exponential_multiply_fusion), channel_id=1, replica_groups=mesh['dp'=8,'branch'=4] {'dp'}, use_global_device_ids=true, to_apply=%region_12.13 | all-reduce | flops 1024 | bytes 8192 | tf_op jit(solution)/shard_map/psum | solution.py:88
  102.2 10.4 %psum.49 = f32[512]{0:T(512)S(1)} all-reduce(f32[512]{0:T(512)S(1)} %exponential_multiply_fusion.1), channel_id=1, replica_groups=mesh['dp'=8,'branch'=4] {'branch'}, use_global_device_ids=true, to_apply=%region_5.6 | all-reduce | flops 512 | bytes 4096 | tf_op jit(solution)/shard_map/psum | solution.py:85
  112.6 4.8 %convolution_multiply_fusion.2 = f32[512,768]{1,0:T(8,128)} fusion(bf16[1024,768]{1,0:T(8,128)(2,1)} %all-gather.2.cloned.1.call-done, f32[]{:T(128)} %bitcast, f32[512,1024]{1,0:T(8,128)} %get-tuple-element.44, f32[1024]{0:T(1024)S(1)} %log_add_fusion, f32[512]{0:T(512)S(1)} %log_add_fusion.1, s32[1024]{0:T(1024)S(1)} %fusion.17, s32[512]{0:T(512)S(1)} %dynamic_slice.20), kind=kOutput, calls=%fused_computation.11 | convolution fusion | flops 809893888 | bytes 5255172 | tf_op jit(solution)/shard_map/dot_general | solution.py:103
  117.5 5.0 %convolution_multiply_fusion = f32[1024,768]{1,0:T(8,128)} fusion(f32[]{:T(128)} %bitcast, bf16[1024,768]{1,0:T(8,128)(2,1)} %constant_dynamic-update-slice_fusion, s32[]{:T(128)S(6)} %select_n.55, f32[512,1024]{1,0:T(8,128)} %get-tuple-element.44, f32[1024]{0:T(1024)S(1)} %log_add_fusion, f32[512]{0:T(512)S(1)} %log_add_fusion.1, s32[1024]{0:T(1024)S(1)} %fusion.17, ...), kind=kOutput, calls=%fused_computation.9 | convolution fusion | flops 810287104 | bytes 6042116 | tf_op jit(solution)/shard_map/dot_general | solution.py:110
  123.2 3.7 %multiply_reduce_fusion = (f32[]{:T(128)}, f32[512]{0:T(512)S(1)}) fusion(f32[512,1024]{1,0:T(8,128)} %get-tuple-element.44, f32[1024]{0:T(1024)S(1)} %log_add_fusion, f32[512]{0:T(512)S(1)} %log_add_fusion.1, s32[1024]{0:T(1024)S(1)} %fusion.17, s32[512]{0:T(512)S(1)} %dynamic_slice.20), kind=kLoop, calls=%fused_computation.5 | loop fusion | flops 5766655 | bytes 2111492 | tf_op jit(solution)/shard_map/reduce_sum | solution.py:99
  126.9 9.1 %psum.50 = f32[512]{0:T(512)S(1)} all-reduce(f32[512]{0:T(512)S(1)} %get-tuple-element.31), channel_id=1, replica_groups=mesh['dp'=8,'branch'=4] {'branch'}, use_global_device_ids=true, to_apply=%region_7.8 | all-reduce | flops 512 | bytes 4096 | tf_op jit(solution)/shard_map/psum | solution.py:85
  136.0 14.5 %reduce-scatter.3.cloned.1.call-done = f32[128,768]{1,0:T(8,128)} async-done(((f32[512,768]{1,0:T(8,128)}), f32[128,768]{1,0:T(8,128)}) %reduce-scatter.3.cloned.1.call-update) | async-done | bytes 393232 | tf_op jit(solution)/shard_map/reduce_scatter | solution.py:101
  152.8 17.9 %all_gather.10 = bf16[512,768]{1,0:T(8,128)(2,1)S(1)} all-gather(bf16[128,768]{1,0:T(8,128)(2,1)S(1)} %divide_convert_fusion.1), channel_id=1, replica_groups=mesh['dp'=8,'branch'=4] {'branch'}, dimensions={0}, use_global_device_ids=true | all-gather | bytes 983040 | tf_op jit(solution)/shard_map/all_gather | solution.py:123
  172.0 26.8 %reduce-scatter.5.cloned.1.call-done = f32[128,768]{1,0:T(8,128)} async-done(((f32[1024,768]{1,0:T(8,128)}), f32[128,768]{1,0:T(8,128)}) %reduce-scatter.5.cloned.1.call-update) | async-done | bytes 393232 | tf_op jit(solution)/shard_map/reduce_scatter | solution.py:108
  201.1 19.6 %all_gather.11 = bf16[512,768]{1,0:T(8,128)(2,1)S(1)} all-gather(bf16[128,768]{1,0:T(8,128)(2,1)S(1)} %divide_convert_fusion), channel_id=1, replica_groups=mesh['dp'=8,'branch'=4] {'branch'}, dimensions={0}, use_global_device_ids=true | all-gather | bytes 983040 | tf_op jit(solution)/shard_map/all_gather | solution.py:124
  223.8 38.5 %all-reduce = (f32[1]{0:T(128)}, f32[1]{0:T(128)}) all-reduce(f32[1]{0:T(128)} %bitcast.6, f32[1]{0:T(128)} %bitcast.7), channel_id=1, replica_groups=mesh['dp'=8,'branch'=4] {'dp','branch'}, use_global_device_ids=true, to_apply=%region_14.15 | all-reduce | flops 2 | bytes 16 | tf_op jit(solution)/shard_map/psum | solution.py:144
  263.4 2.0 convolution_convert_fusion.1
  265.5 14.0 %all-reduce.4.cloned.1.call-done = (f32[256,768]{0,1:T(8,128)}, f32[192,768]{1,0:T(8,128)}) async-done(((f32[256,768]{0,1:T(8,128)}, f32[192,768]{1,0:T(8,128)}), (f32[256,768]{0,1:T(8,128)}, f32[192,768]{1,0:T(8,128)})) %all-reduce.4.cloned.1.call-update) | async-done | bytes 1376272 | tf_op jit(solution)/shard_map/psum | solution.py:138
  279.5 2.3 copy.19
  (51 shorter events, 22.8 us)
Async XLA Ops:
  7.2 26.4 %copy-start = (bf16[1024,768]{1,0:T(8,128)(2,1)S(1)}, bf16[1024,768]{1,0:T(8,128)(2,1)}, u32[]{:S(2)}) copy-start(bf16[1024,768]{1,0:T(8,128)(2,1)} %param.8) | copy-start | bytes 4718596
  21.9 11.5 %all-to-all-start = ((bf16[4,128,256]{2,1,0:T(8,128)(2,1)}), bf16[4,128,256]{2,1,0:T(8,128)(2,1)S(1)}, u32[]{:S(2)}, u32[]{:S(2)}) async-start(bf16[4,128,256]{2,1,0:T(8,128)(2,1)} %bitcast.30), calls=%async_computation | async-start | bytes 524288 | tf_op jit(solution)/shard_map/all_to_all | solution.py:32
  25.3 38.5 %all-gather.2.cloned.1.call-start = ((), (), s32[]{:S(2)}) async-start(), calls=%async_computation.4 | async-start | bytes 1769472 | tf_op jit(solution)/shard_map/all_gather | solution.py:56
  27.9 122.6 %reduce-scatter.3.cloned.1.call-start = ((), (), s32[]{:S(2)}) async-start(), calls=%async_computation.5 | async-start | bytes 1966080 | tf_op jit(solution)/shard_map/reduce_scatter | solution.py:101
  34.2 7.6 %collective-permute-start = (bf16[128,768]{1,0:T(8,128)(2,1)S(1)}, bf16[128,768]{1,0:T(8,128)(2,1)S(1)}, u32[]{:S(2)}, u32[]{:S(2)}) collective-permute-start(bf16[128,768]{1,0:T(8,128)(2,1)S(1)} %fusion.23), channel_id=1, source_target_pairs={{0,1},{1,2},{2,3},{3,0},{4,5},{5,6},{6,7},{7,4},{8,9},{9,10},{10,1... | collective-permute-start | bytes 589832 | tf_op jit(solution)/shard_map/ppermute | solution.py:45
  41.9 8.7 %collective-permute-start.1 = (bf16[128,768]{1,0:T(8,128)(2,1)S(1)}, bf16[128,768]{1,0:T(8,128)(2,1)S(1)}, u32[]{:S(2)}, u32[]{:S(2)}) collective-permute-start(bf16[128,768]{1,0:T(8,128)(2,1)S(1)} %collective-permute-done), channel_id=1, source_target_pairs={{0,1},{1,2},{2,3},{3,0},{4,5},{5,6},{6,7},{7,4},{8,9},{9,10},{10,1... | collective-permute-start | bytes 589832 | tf_op jit(solution)/shard_map/ppermute | solution.py:45
  50.6 7.5 %collective-permute-start.2 = (bf16[128,768]{1,0:T(8,128)(2,1)S(1)}, bf16[128,768]{1,0:T(8,128)(2,1)S(1)}, u32[]{:S(2)}, u32[]{:S(2)}) collective-permute-start(bf16[128,768]{1,0:T(8,128)(2,1)S(1)} %collective-permute-done.1), channel_id=1, source_target_pairs={{0,1},{1,2},{2,3},{3,0},{4,5},{5,6},{6,7},{7,4},{8,9},{9,10},{10,1... | collective-permute-start | bytes 589832 | tf_op jit(solution)/shard_map/ppermute | solution.py:45
  117.4 81.4 %reduce-scatter.5.cloned.1.call-start = ((), (), s32[]{:S(2)}) async-start(), calls=%async_computation.6 | async-start | bytes 3538944 | tf_op jit(solution)/shard_map/reduce_scatter | solution.py:108
  122.5 157.0 %all-reduce.4.cloned.1.call-start = ((), (), s32[]{:S(2)}) async-start(), calls=%async_computation.7 | async-start | bytes 2752512 | tf_op jit(solution)/shard_map/psum | solution.py:138
  123.2 47.5 %copy-start.1 = (bf16[512,256]{1,0:T(8,128)(2,1)S(1)}, bf16[512,256]{1,0:T(8,128)(2,1)}, u32[]{:S(2)}) copy-start(bf16[512,256]{1,0:T(8,128)(2,1)} %param.6) | copy-start | bytes 786436
  172.0 48.7 %copy-start.2 = (bf16[512,192]{0,1:T(8,128)(2,1)S(1)}, bf16[512,192]{0,1:T(8,128)(2,1)}, u32[]{:S(2)}) copy-start(bf16[512,192]{0,1:T(8,128)(2,1)} %param.7) | copy-start | bytes 589828
Sparse Core Ops, SparseCore 0:
  28.6 26.9 all-gather.1
  117.6 32.8 reduce-scatter.2
  153.9 44.8 reduce-scatter.4
  222.0 57.4 all-reduce.3
